TPU v7x, 32 devices: a whole 2x2x4 slice. The times are simulated.
32 devices in a mesh: row: 16 (over z, y, x), col: 2 (over core).
Axes of the slice: x: 2, y: 2, z: 4, core: 2. Of those that a mesh axis runs over, the one named last changes fastest.
Arguments:
- incident: bfloat16 [2, 8192, 512], P(None, ('row', 'col')), may hold values from -6 to 6
- near_tiles: bfloat16 [32, 2, 3, 2, 256, 256], P(('row', 'col')), may hold values from -0.15625 to 0.15625
- near_offsets: int32 [32, 3], P(('row', 'col')), may hold values from -2 to 2, as said below
- far_row: int32 [16, 2, 16], P('row', 'col'), may hold values from 0 to 1, as said below
- far_col: int32 [16, 2, 16], P('row', 'col'), may hold values from 0 to 15
- far_rank: int32 [16, 2, 16], P('row', 'col'), may hold values from 8 to 32, as said below
- far_count: int32 [16, 2], P('row', 'col'), may hold values from 2 to 16, as said below
- far_u: bfloat16 [16, 2, 2, 16, 2, 32, 256], P('row', 'col'), may hold values from -0.25 to 0.25
- far_v: bfloat16 [16, 2, 2, 16, 2, 32, 256], P('row', 'col'), may hold values from -0.25 to 0.25
Outputs:
- response: bfloat16 [2, 8192, 512], P(None, ('row', 'col'))
Inputs may be any that keep to these rules, and one draw needn't show every extreme that they name: `near_offsets`: slot 0 of every tile is 0; the other slots of a tile hold distinct values among -2, -1, 1, 2. On one device the pairs (far_row, far_col) of all 16 slots are distinct, and every block (i, j) they name has circular tile distance 3 or more between i and j. `far_rank`: slot 0 of every device has rank 32. `far_count`: some device has all 16 slots live.
All inputs are finite; a program needn't handle non-finite values.
Results may differ from a plain program's by a relative error of at most 0.0035.
Values may be sent and summed in bfloat16 or wider, within the bound.
A program may use at most 192 MiB of HBM per device.

v0:
```python
import functools

import jax
import jax.numpy as jnp
from jax import lax
from jax.experimental import pallas as pl
from jax.experimental.pallas import tpu as pltpu
from jax.sharding import PartitionSpec as P

MESH = pl.DeviceIdType.MESH
UP, DOWN, ALONG_Y, ALONG_X = range(4)


def from_behind(value, axis, steps):
    count = lax.axis_size(axis)
    pairs = [(source, (source + steps) % count) for source in range(count)]
    return lax.ppermute(value, axis, pairs)


def combine_parts(real_prod, imag_prod):
    half_width = real_prod.shape[-1] // 2
    return jnp.concatenate(
        [
            real_prod[..., :half_width] - imag_prod[..., half_width:],
            real_prod[..., half_width:] + imag_prod[..., :half_width],
        ],
        axis=-1,
    )


def far_partial(
    wave_tiles,
    rows_local,
    cols_local,
    rank_local,
    live_count,
    u_wave,
    v_wave,
    group_limit,
    row_blocks,
):
    group_size = 16
    tile_rows = wave_tiles.shape[1]
    columns = wave_tiles.shape[2]
    rank_size = v_wave.shape[2]
    slot_ids = jnp.arange(group_size, dtype=jnp.int32)
    rank_ids = jnp.arange(rank_size, dtype=jnp.int32)

    def add_group(group_step, far_sum):
        first_slot = group_step * group_size
        rows_group = lax.dynamic_slice_in_dim(rows_local, first_slot, group_size)
        cols_group = lax.dynamic_slice_in_dim(cols_local, first_slot, group_size)
        rank_group = lax.dynamic_slice_in_dim(rank_local, first_slot, group_size)
        v_group = lax.dynamic_slice_in_dim(v_wave, first_slot, group_size, 0)
        u_group = lax.dynamic_slice_in_dim(u_wave, first_slot, group_size, 0)
        slot_tiles = jnp.take(wave_tiles, cols_group, axis=0)
        real_prod = jnp.einsum(
            "fkq,fqc->fkc", v_group[:, 0], slot_tiles, preferred_element_type=jnp.float32
        )
        imag_prod = jnp.einsum(
            "fkq,fqc->fkc", v_group[:, 1], slot_tiles, preferred_element_type=jnp.float32
        )
        live_mask = (first_slot + slot_ids < live_count)[:, None] & (
            rank_ids[None, :] < rank_group[:, None]
        )
        coefficients = (
            combine_parts(real_prod, imag_prod) * live_mask[:, :, None].astype(jnp.float32)
        ).astype(jnp.bfloat16)
        real_back = jnp.einsum(
            "fkp,fkc->fpc", u_group[:, 0], coefficients, preferred_element_type=jnp.float32
        )
        imag_back = jnp.einsum(
            "fkp,fkc->fpc", u_group[:, 1], coefficients, preferred_element_type=jnp.float32
        )
        contrib = combine_parts(real_back, imag_back)
        return far_sum.at[rows_group].add(contrib)

    zero_sum = jnp.zeros((row_blocks, tile_rows, columns), jnp.float32)
    return lax.fori_loop(0, group_limit, add_group, zero_sum)


def reduce_rows(far_sum, row_blocks, tile_rows, columns):
    flat_rows = far_sum.reshape(row_blocks * tile_rows, columns)
    return lax.psum_scatter(flat_rows, "col", scatter_dimension=0, tiled=True)


def generic_shards(incident, near_tiles, near_offsets, far_row, far_col, far_rank, far_count, far_u, far_v):
    wave_count, tile_rows, columns = incident.shape
    row_blocks = lax.axis_size("col")
    slot_count = far_row.shape[2]
    stacked = []
    for shift_by in (2, 1, 0, -1, -2):
        if shift_by == 0:
            stacked.append(incident)
        else:
            stacked.append(from_behind(incident, ("row", "col"), shift_by))
    neighbour = jnp.stack(stacked, axis=1)
    near_inputs = jnp.take(neighbour, near_offsets[0] + 2, axis=1)
    local_near = near_tiles[0]
    real_prod = jnp.einsum(
        "wnpq,wnqc->wpc", local_near[:, :, 0], near_inputs, preferred_element_type=jnp.float32
    )
    imag_prod = jnp.einsum(
        "wnpq,wnqc->wpc", local_near[:, :, 1], near_inputs, preferred_element_type=jnp.float32
    )
    near_total = combine_parts(real_prod, imag_prod)
    rows_local = far_row[0, 0]
    cols_local = far_col[0, 0]
    rank_local = far_rank[0, 0]
    live_count = far_count[0, 0]
    group_limit = slot_count // 16
    gathered = lax.all_gather(incident, "row", axis=1, tiled=True)
    outputs = []
    for wave_index in range(wave_count):
        wave_columns = gathered[wave_index]
        wave_tiles = wave_columns.reshape(-1, tile_rows, columns)
        far_sum = far_partial(
            wave_tiles,
            rows_local,
            cols_local,
            rank_local,
            live_count,
            far_u[0, 0, wave_index],
            far_v[0, 0, wave_index],
            group_limit,
            row_blocks,
        )
        own_rows = reduce_rows(far_sum, row_blocks, tile_rows, columns)
        outputs.append(near_total[wave_index] + own_rows)
    return jnp.stack(outputs, axis=0).astype(jnp.bfloat16)


def turned(block):
    half = block.shape[-1] // 2
    return jnp.concatenate([-block[:, half:], block[:, :half]], axis=-1)


def fused_kernel(
    depth, slot_ref, offset_ref, x_ref, near_hbm, u_hbm, v_hbm, out_ref,
    tiles, near_buf, u_buf, v_buf, u_dense, coef, v_out, v_in, coef_out, outgoing, incoming, total,
    recv_sem, send_sem, pair_sem, v_send, v_recv, c_send, c_recv, sum_send, sum_recv, load_sem,
):
    waves = x_ref.shape[0]
    row_count = depth * 4
    row_blocks = slot_ref.shape[1]
    rank_rows = v_buf.shape[3]
    r = lax.axis_index("row")
    c = lax.axis_index("col")
    z, y, x = r // 4, (r // 2) % 2, r % 2
    own_slot, edge_slot = row_count, row_count + 1
    edge_tile = (r + 1 - 2 * c + row_count) % row_count
    side = 2 * x - 1
    partner = r + 2 * (1 - 2 * y)
    corner = (r + side + row_count) % row_count
    partner_corner = (partner + side + row_count) % row_count

    def row_of(tz, ty, tx):
        return (tz * 2 + ty) * 2 + tx

    loads = [
        pltpu.make_async_copy(v_hbm.at[0, 0], v_buf, load_sem.at[0]),
        pltpu.make_async_copy(u_hbm.at[0, 0], u_buf, load_sem.at[1]),
        pltpu.make_async_copy(near_hbm.at[0], near_buf, load_sem.at[2]),
    ]
    for load in loads:
        load.start()

    barrier = pltpu.get_barrier_semaphore()
    greeted = (
        (row_of((z + 1) % depth, y, x), c),
        (row_of((z + depth - 1) % depth, y, x), c),
        (partner, c),
        (row_of(z, y, 1 - x), c),
        (r, 1 - c),
    )
    for device in greeted:
        pl.semaphore_signal(barrier, inc=1, device_id=device, device_id_type=MESH)
    pl.semaphore_wait(barrier, len(greeted))

    def copy_to(source, target, sent, received, device):
        return pltpu.make_async_remote_copy(
            src_ref=source,
            dst_ref=target,
            send_sem=sent,
            recv_sem=received,
            device_id=device,
            device_id_type=MESH,
        )

    def hop(wave, tile, link, row, source=None):
        here = tiles.at[wave, tile]
        return copy_to(
            here if source is None else source,
            here,
            send_sem.at[wave, tile, link],
            recv_sem.at[wave, tile],
            (row, c),
        )

    def along_z(wave, tile, step, source=None):
        target = (z + step + depth) % depth
        return hop(wave, tile, (1 - step) // 2, row_of(target, y, x), source)

    def along_x(wave, tile, source=None):
        return hop(wave, tile, ALONG_X, row_of(z, y, 1 - x), source)

    def along_y(wave, tile, source=None):
        return hop(wave, tile, ALONG_Y, partner, source)

    def to_pair(wave, source, slot):
        return copy_to(
            source,
            tiles.at[wave, slot],
            pair_sem.at[wave, slot - row_count],
            recv_sem.at[wave, slot],
            (r, 1 - c),
        )

    def send_v(place):
        return copy_to(
            v_out.at[place], v_in.at[place], v_send.at[place], v_recv.at[place], (partner, c)
        )

    def send_coef(place, tile):
        return copy_to(
            coef_out.at[place], coef.at[0, tile], c_send.at[place], c_recv.at[place], (partner, c)
        )

    rank_ids = lax.broadcasted_iota(jnp.int32, (rank_rows, v_buf.shape[4]), 0)

    def complex_rows(prod, a):
        at = 2 * rank_rows * a
        return combine_parts(prod[at:at + rank_rows], prod[at + rank_rows:at + 2 * rank_rows])

    def project(wave, tile):
        block = tiles[wave, tile]
        factors = [
            v_buf[wave, slot_ref[0, a, tile]].reshape(2 * rank_rows, -1) for a in range(row_blocks)
        ]
        prod = jnp.dot(
            jnp.concatenate(factors, axis=0), block, preferred_element_type=jnp.float32
        )
        ids = lax.broadcasted_iota(jnp.int32, (rank_rows, block.shape[1]), 0)
        for a in range(row_blocks):
            both = jnp.where(ids < slot_ref[1, a, tile], complex_rows(prod, a), 0.0)
            coef[0, tile, wave, a] = both.astype(jnp.bfloat16)
            coef[1, tile, wave, a] = turned(both).astype(jnp.bfloat16)

    def serve(place, tile):
        for wave in range(waves):
            left = v_in[place, wave].reshape(row_blocks * 2 * rank_rows, -1)
            prod = jnp.dot(left, tiles[wave, tile], preferred_element_type=jnp.float32)
            for a in range(row_blocks):
                coef_out[place, wave, a] = complex_rows(prod, a).astype(jnp.bfloat16)

    def use_tile(level, tx):
        tile, place = row_of(level, y, tx), level * 2 + tx

        @pl.when(tile == partner_corner)
        def _():
            for wave in range(waves):
                along_y(wave, tile).start()

        @pl.when(tile != partner_corner)
        def _():
            send_v(place).wait_recv()
            serve(place, tile)

        for wave in range(waves):
            project(wave, tile)

        @pl.when(tile != partner_corner)
        def _():
            send_coef(place, tile).start()

    def arrive(wave, tile):
        pltpu.make_async_copy(tiles.at[wave, tile], tiles.at[wave, tile], recv_sem.at[wave, tile]).wait()

    def share_edge(wave, tile):
        @pl.when(tile == edge_tile)
        def _():
            to_pair(wave, tiles.at[wave, tile], edge_slot).start()

    lag = 2

    def level_of(step):
        sign = 1 - 2 * (step % 2)
        return (z + sign * ((step + 1) // 2) + depth) % depth, sign

    def reach(wave, step):
        return depth // 2 if (step == 1) == (wave % 2 == 0) else (depth - 1) // 2

    for wave in range(waves):
        own = x_ref.at[wave]
        along_x(wave, r, own).start()
        for step in (1, -1):
            if reach(wave, step) > 0:
                along_z(wave, r, step, own).start()
        to_pair(wave, own, own_slot).start()
        tiles[wave, r] = x_ref[wave]

    loads[0].wait()

    def place_v(place, carry):
        tile = row_of(place // 2, 1 - y, place % 2)
        for wave in range(waves):
            for a in range(row_blocks):
                factor = v_buf[wave, slot_ref[0, a, tile]]
                for part in range(2):
                    kept = factor[part].astype(jnp.float32)
                    kept = jnp.where(rank_ids < slot_ref[1, a, tile], kept, 0.0)
                    v_out[place, wave, a, part] = kept.astype(jnp.bfloat16)
        return carry

    lax.fori_loop(0, 2 * depth, place_v, 0)

    def push_v(step, carry):
        level, _ = level_of(step // 2)
        tx = (x + step) % 2

        @pl.when(row_of(level, 1 - y, tx) != corner)
        def _():
            send_v(level * 2 + tx).start()

        return carry

    lax.fori_loop(0, 2 * depth, push_v, 0)

    for load in loads[1:]:
        load.wait()

    def place_u(tile, carry):
        for wave in range(waves):
            for a in range(row_blocks):
                factor = u_buf[wave, slot_ref[0, a, tile]]
                u_dense[wave, a, 0, tile] = factor[0]
                u_dense[wave, a, 1, tile] = factor[1]
        return carry

    lax.fori_loop(0, row_count, place_u, 0)

    def spread(step, carry):
        level, sign = level_of(step)

        @pl.when(step < depth)
        def _():
            tile = row_of(level, y, x)

            @pl.when(step > 0)
            def _():
                for wave in range(waves):
                    arrive(wave, tile)

                    for move in (1, -1):
                        @pl.when((sign == -move) & ((step + 1) // 2 < reach(wave, move)))
                        def _():
                            along_z(wave, tile, move).start()

                    along_x(wave, tile).start()

            use_tile(level, x)

        behind, _ = level_of(jnp.maximum(step - lag, 0))

        @pl.when(step >= lag)
        def _():
            tile = row_of(behind, y, 1 - x)
            for wave in range(waves):
                arrive(wave, tile)
                share_edge(wave, tile)
            use_tile(behind, 1 - x)

        return carry

    lax.fori_loop(0, depth + lag, spread, 0)

    for wave in range(waves):
        arrive(wave, corner)
        share_edge(wave, corner)
        project(wave, corner)

    def finish(place, carry):
        tile = row_of(place // 2, 1 - y, place % 2)

        @pl.when(tile != corner)
        def _():
            send_coef(place, tile).wait_recv()
            for wave in range(waves):
                for a in range(row_blocks):
                    coef[1, tile, wave, a] = turned(coef[0, tile, wave, a])

        return carry

    lax.fori_loop(0, 2 * depth, finish, 0)

    def far_sum(wave, a):
        left = u_dense[wave, a].reshape(-1, u_dense.shape[-1])
        right = coef[:, :, wave, a].reshape(-1, coef.shape[-1])
        return lax.dot_general(
            left, right, (((0,), (0,)), ((), ())), preferred_element_type=jnp.float32
        )

    def send_sum(wave):
        return copy_to(
            outgoing.at[wave], incoming.at[wave], sum_send.at[wave], sum_recv.at[wave], (r, 1 - c)
        )

    def fill(wave, carry):
        outgoing[wave] = far_sum(wave, 1 - c)
        return carry

    lax.fori_loop(0, waves, fill, 0)
    for wave in range(waves):
        arrive(wave, own_slot)
        arrive(wave, edge_slot)

    def place_of(offset):
        even = (r + offset // 2 + row_count) % row_count
        same_chip = offset == 1 - 2 * c
        return jnp.where(offset % 2 == 0, even, jnp.where(same_chip, own_slot, edge_slot))

    def own_rows(wave, carry):
        send_sum(wave).start()
        value = far_sum(wave, c)
        for n in range(near_buf.shape[1]):
            block = tiles[wave, place_of(offset_ref[n])]
            value += jnp.dot(near_buf[wave, n, 0], block, preferred_element_type=jnp.float32)
            value += jnp.dot(
                near_buf[wave, n, 1], turned(block), preferred_element_type=jnp.float32
            )
        total[wave] = value
        return carry

    lax.fori_loop(0, waves, own_rows, 0)
    for wave in range(waves):
        send_sum(wave).wait()
        out_ref[wave] = (total[wave] + incoming[wave]).astype(out_ref.dtype)

    for wave in range(waves):
        to_pair(wave, x_ref.at[wave], own_slot).wait_send()
        to_pair(wave, x_ref.at[wave], edge_slot).wait_send()
        along_y(wave, partner_corner).wait_send()

    def drain(level, carry):
        tile = row_of(level, y, x)
        for wave in range(waves):
            along_x(wave, tile).wait_send()
            for move in (1, -1):
                @pl.when((move * (z - level) + depth) % depth < reach(wave, move))
                def _():
                    along_z(wave, tile, move).wait_send()

        for tx in range(2):
            place = level * 2 + tx

            @pl.when(row_of(level, 1 - y, tx) != corner)
            def _():
                send_v(place).wait_send()

            @pl.when(row_of(level, y, tx) != partner_corner)
            def _():
                send_coef(place, row_of(level, y, tx)).wait_send()
        return carry

    lax.fori_loop(0, depth, drain, 0)


def fused_shards(incident, near_tiles, near_offsets, far_row, far_col, far_rank, far_count, far_u, far_v):
    waves, tile_rows, columns = incident.shape
    row_count, row_blocks = lax.axis_size("row"), lax.axis_size("col")
    slots, rank_rows = far_u.shape[3], far_u.shape[5]
    near_slots = near_tiles.shape[2]
    slot_ids = jnp.arange(slots, dtype=jnp.int32)
    block_key = far_row[0, 0] * row_count + far_col[0, 0]
    live = slot_ids < far_count[0, 0]
    match = (block_key[:, None] == jnp.arange(row_blocks * row_count, dtype=jnp.int32)[None, :]) & live[:, None]
    stacked = jnp.stack([slot_ids, far_rank[0, 0]], axis=0)
    table = jnp.sum(jnp.where(match[None], stacked[:, :, None], 0), axis=1)
    table = table.reshape(2, row_blocks, row_count)
    bf16, f32 = jnp.bfloat16, jnp.float32
    any_space = pl.BlockSpec(memory_space=pl.ANY)
    smem = pl.BlockSpec(memory_space=pltpu.SMEM)
    vmem = pl.BlockSpec(memory_space=pltpu.VMEM)
    dma = pltpu.SemaphoreType.DMA
    return pl.pallas_call(
        functools.partial(fused_kernel, row_count // 4),
        out_shape=jax.ShapeDtypeStruct(incident.shape, bf16),
        in_specs=[smem, smem, vmem, any_space, any_space, any_space],
        out_specs=vmem,
        scratch_shapes=[
            pltpu.VMEM((waves, row_count + 2, tile_rows, columns), bf16),
            pltpu.VMEM((waves, near_slots, 2, tile_rows, tile_rows), bf16),
            pltpu.VMEM((waves, slots, 2, rank_rows, tile_rows), bf16),
            pltpu.VMEM((waves, slots, 2, rank_rows, tile_rows), bf16),
            pltpu.VMEM((waves, row_blocks, 2, row_count, rank_rows, tile_rows), bf16),
            pltpu.VMEM((2, row_count, waves, row_blocks, rank_rows, columns), bf16),
            pltpu.VMEM((row_count // 2, waves, row_blocks, 2, rank_rows, tile_rows), bf16),
            pltpu.VMEM((row_count // 2, waves, row_blocks, 2, rank_rows, tile_rows), bf16),
            pltpu.VMEM((row_count // 2, waves, row_blocks, rank_rows, columns), bf16),
            pltpu.VMEM((waves, tile_rows, columns), f32),
            pltpu.VMEM((waves, tile_rows, columns), f32),
            pltpu.VMEM((waves, tile_rows, columns), f32),
            dma((waves, row_count + 2)),
            dma((waves, row_count, 4)),
            dma((waves, 2)),
            dma((row_count // 2,)),
            dma((row_count // 2,)),
            dma((row_count // 2,)),
            dma((row_count // 2,)),
            dma((waves,)),
            dma((waves,)),
            dma((3,)),
        ],
        compiler_params=pltpu.CompilerParams(collective_id=0, has_side_effects=True),
    )(table, near_offsets[0], incident, near_tiles, far_u, far_v)


def solution(mesh):
    in_specs = (
        P(None, ("row", "col"), None),
        P(("row", "col"), None, None, None, None, None),
        P(("row", "col"), None),
        P("row", "col", None),
        P("row", "col", None),
        P("row", "col", None),
        P("row", "col"),
        P("row", "col", None, None, None, None, None),
        P("row", "col", None, None, None, None, None),
    )
    out_specs = P(None, ("row", "col"), None)
    paired = mesh.shape["col"] == 2 and mesh.shape["row"] % 4 == 0 and mesh.shape["row"] > 4
    shards = fused_shards if paired else generic_shards
    return jax.shard_map(shards, mesh=mesh, in_specs=in_specs, out_specs=out_specs, check_vma=False)
```

profile of v0, /device:TPU:0, one launch (start us, length us, event | category | flops | bytes accessed | tf_op | source)
XLA Modules:
  0.0 73.8 jit_solution(13702490109383889211)
XLA Ops:
  0.7 0.7 add_bitcast_fusion
  1.3 0.7 pad_add_fusion
  2.0 0.1 fusion
  2.1 0.1 select_reduce_fusion
  2.2 0.7 reshape.53.slot_ref
  2.8 69.1 %shard_map.91 = bf16[2,256,512]{2,1,0:T(8,128)(2,1)} custom-call(s32[2,2,16]{2,1,0:T(2,128)} %reshape.53.slot_ref, s32[3]{0:T(128)} %bitcast.6, bf16[2,256,512]{2,1,0:T(8,128)(2,1)} %x_ref.1, bf16[1,2,3,2,256,256]{5,4,3,2,1,0:T(8,128)(2,1)} %near_hbm.1, bf16[1,1,2,16,2,32,256]{6,5,4,3,2,1,0:T(8,128)(2,1)} %u_hbm.1, bf16[1,1,2,16,2,32,256]{6,5,4,3,2,1,0:T(8,128)(2,1)} %v_hbm.1), custom_call_target="tpu_custom_call" | custom-call | tf_op jit(solution)/shard_map/pallas_call | solution.py:485
  71.9 1.9 %copy.12 = bf16[2,256,512]{2,1,0:T(8,128)(2,1)} copy(bf16[2,256,512]{2,1,0:T(8,128)(2,1)} %shard_map.91) | data formatting | bytes 1048576
  (2 shorter events, 0.0 us)
where the time goes:
time: 74 us; the launch traced here: 73.8 us
  Pallas kernels  69.1 us (93%)
  local copies, waits for them, and re-layouts  2.53 us (3%)
  other arithmetic  1.51 us (2%)
    pallas_call x1, Pallas kernels, fused_shards(): pl.pallas_call(functools.partial(fused_kernel, row_count // 4), out_shape...  69.1 us
    unnamed x1, local copies, waits for them, and re-layouts  1.87 us

commit v1 on v0

v1 whole, which is shorter than its diff:
```python
import functools

import jax
import jax.numpy as jnp
from jax import lax
from jax.experimental import pallas as pl
from jax.experimental.pallas import tpu as pltpu
from jax.sharding import PartitionSpec as P

MESH = pl.DeviceIdType.MESH
UP, DOWN, ALONG_Y, ALONG_X = range(4)


def from_behind(value, axis, steps):
    count = lax.axis_size(axis)
    pairs = [(source, (source + steps) % count) for source in range(count)]
    return lax.ppermute(value, axis, pairs)


def combine_parts(real_prod, imag_prod):
    half_width = real_prod.shape[-1] // 2
    return jnp.concatenate(
        [
            real_prod[..., :half_width] - imag_prod[..., half_width:],
            real_prod[..., half_width:] + imag_prod[..., :half_width],
        ],
        axis=-1,
    )


def far_partial(
    wave_tiles,
    rows_local,
    cols_local,
    rank_local,
    live_count,
    u_wave,
    v_wave,
    group_limit,
    row_blocks,
):
    group_size = 16
    tile_rows = wave_tiles.shape[1]
    columns = wave_tiles.shape[2]
    rank_size = v_wave.shape[2]
    slot_ids = jnp.arange(group_size, dtype=jnp.int32)
    rank_ids = jnp.arange(rank_size, dtype=jnp.int32)

    def add_group(group_step, far_sum):
        first_slot = group_step * group_size
        rows_group = lax.dynamic_slice_in_dim(rows_local, first_slot, group_size)
        cols_group = lax.dynamic_slice_in_dim(cols_local, first_slot, group_size)
        rank_group = lax.dynamic_slice_in_dim(rank_local, first_slot, group_size)
        v_group = lax.dynamic_slice_in_dim(v_wave, first_slot, group_size, 0)
        u_group = lax.dynamic_slice_in_dim(u_wave, first_slot, group_size, 0)
        slot_tiles = jnp.take(wave_tiles, cols_group, axis=0)
        real_prod = jnp.einsum(
            "fkq,fqc->fkc", v_group[:, 0], slot_tiles, preferred_element_type=jnp.float32
        )
        imag_prod = jnp.einsum(
            "fkq,fqc->fkc", v_group[:, 1], slot_tiles, preferred_element_type=jnp.float32
        )
        live_mask = (first_slot + slot_ids < live_count)[:, None] & (
            rank_ids[None, :] < rank_group[:, None]
        )
        coefficients = (
            combine_parts(real_prod, imag_prod) * live_mask[:, :, None].astype(jnp.float32)
        ).astype(jnp.bfloat16)
        real_back = jnp.einsum(
            "fkp,fkc->fpc", u_group[:, 0], coefficients, preferred_element_type=jnp.float32
        )
        imag_back = jnp.einsum(
            "fkp,fkc->fpc", u_group[:, 1], coefficients, preferred_element_type=jnp.float32
        )
        contrib = combine_parts(real_back, imag_back)
        return far_sum.at[rows_group].add(contrib)

    zero_sum = jnp.zeros((row_blocks, tile_rows, columns), jnp.float32)
    return lax.fori_loop(0, group_limit, add_group, zero_sum)


def reduce_rows(far_sum, row_blocks, tile_rows, columns):
    flat_rows = far_sum.reshape(row_blocks * tile_rows, columns)
    return lax.psum_scatter(flat_rows, "col", scatter_dimension=0, tiled=True)


def generic_shards(incident, near_tiles, near_offsets, far_row, far_col, far_rank, far_count, far_u, far_v):
    wave_count, tile_rows, columns = incident.shape
    row_blocks = lax.axis_size("col")
    slot_count = far_row.shape[2]
    stacked = []
    for shift_by in (2, 1, 0, -1, -2):
        if shift_by == 0:
            stacked.append(incident)
        else:
            stacked.append(from_behind(incident, ("row", "col"), shift_by))
    neighbour = jnp.stack(stacked, axis=1)
    near_inputs = jnp.take(neighbour, near_offsets[0] + 2, axis=1)
    local_near = near_tiles[0]
    real_prod = jnp.einsum(
        "wnpq,wnqc->wpc", local_near[:, :, 0], near_inputs, preferred_element_type=jnp.float32
    )
    imag_prod = jnp.einsum(
        "wnpq,wnqc->wpc", local_near[:, :, 1], near_inputs, preferred_element_type=jnp.float32
    )
    near_total = combine_parts(real_prod, imag_prod)
    rows_local = far_row[0, 0]
    cols_local = far_col[0, 0]
    rank_local = far_rank[0, 0]
    live_count = far_count[0, 0]
    group_limit = slot_count // 16
    gathered = lax.all_gather(incident, "row", axis=1, tiled=True)
    outputs = []
    for wave_index in range(wave_count):
        wave_columns = gathered[wave_index]
        wave_tiles = wave_columns.reshape(-1, tile_rows, columns)
        far_sum = far_partial(
            wave_tiles,
            rows_local,
            cols_local,
            rank_local,
            live_count,
            far_u[0, 0, wave_index],
            far_v[0, 0, wave_index],
            group_limit,
            row_blocks,
        )
        own_rows = reduce_rows(far_sum, row_blocks, tile_rows, columns)
        outputs.append(near_total[wave_index] + own_rows)
    return jnp.stack(outputs, axis=0).astype(jnp.bfloat16)


def fused_kernel(
    depth, offset_ref, row_ref, col_ref, rank_ref, count_ref, x_hbm, near_hbm, u_hbm, v_hbm, out_ref,
    tiles, near_buf, u_buf, v_buf, u_turn, u_give, coef, give, v_out, v_in, served, total, keys, table,
    recv_sem, send_sem, pair_sem, v_send, v_recv, s_send, s_recv, g_send, g_recv, t_send, t_recv, load_sem,
):
    waves = tiles.shape[0]
    row_count = depth * 4
    places = depth * 2
    half = depth // 2
    row_blocks = table.shape[1]
    slots = v_buf.shape[1]
    rank_rows = v_buf.shape[3]
    tile_rows = tiles.shape[2]
    r = lax.axis_index("row")
    c = lax.axis_index("col")
    z, y, x = r // 4, (r // 2) % 2, r % 2
    own_slot, edge_slot = row_count, row_count + 1
    edge_tile = (r + 1 - 2 * c + row_count) % row_count
    side = 2 * x - 1
    partner = r + 2 * (1 - 2 * y)
    corner = (r + side + row_count) % row_count
    partner_corner = (partner + side + row_count) % row_count
    has_up, has_down = z < depth - 1, z > 0

    def row_of(tz, ty, tx):
        return (tz * 2 + ty) * 2 + tx

    load_x = [
        pltpu.make_async_copy(x_hbm.at[wave], tiles.at[wave, r], load_sem.at[3 + wave])
        for wave in range(waves)
    ]
    load_v = pltpu.make_async_copy(v_hbm.at[0, 0], v_buf, load_sem.at[0])
    load_u = pltpu.make_async_copy(u_hbm.at[0, 0], u_buf, load_sem.at[1])
    load_near = pltpu.make_async_copy(near_hbm.at[0], near_buf, load_sem.at[2])
    for load in load_x + [load_v, load_u, load_near]:
        load.start()

    barrier = pltpu.get_barrier_semaphore()

    def greet(device):
        pl.semaphore_signal(barrier, inc=1, device_id=device, device_id_type=MESH)

    for device in ((partner, c), (partner, 1 - c), (row_of(z, y, 1 - x), c), (r, 1 - c)):
        greet(device)

    @pl.when(has_up)
    def _():
        greet((row_of(z + 1, y, x), c))

    @pl.when(has_down)
    def _():
        greet((row_of(z - 1, y, x), c))

    for s in range(slots):
        key = row_ref[0, 0, s] * row_count + col_ref[0, 0, s]
        keys[s] = jnp.where(s < count_ref[0, 0], key, -1)

    def look_up(a, tile):
        wanted = a * row_count + tile
        slot, rank = jnp.int32(0), jnp.int32(0)
        for s in range(slots):
            hit = keys[s] == wanted
            slot = jnp.where(hit, s, slot)
            rank = jnp.where(hit, rank_ref[0, 0, s], rank)
        table[0, a, tile] = slot
        table[1, a, tile] = rank

    pl.semaphore_wait(barrier, 4 + jnp.where(has_up, 1, 0) + jnp.where(has_down, 1, 0))

    def copy_to(source, target, sent, received, device):
        return pltpu.make_async_remote_copy(
            src_ref=source,
            dst_ref=target,
            send_sem=sent,
            recv_sem=received,
            device_id=device,
            device_id_type=MESH,
        )

    def hop(wave, tile, link, row):
        here = tiles.at[wave, tile]
        return copy_to(here, here, send_sem.at[wave, tile, link], recv_sem.at[wave, tile], (row, c))

    def along_z(wave, tile, step):
        return hop(wave, tile, (1 - step) // 2, row_of(z + step, y, x))

    def along_x(wave, tile):
        return hop(wave, tile, ALONG_X, row_of(z, y, 1 - x))

    def along_y(wave, tile):
        return hop(wave, tile, ALONG_Y, partner)

    def to_pair(wave, tile, slot):
        return copy_to(
            tiles.at[wave, tile],
            tiles.at[wave, slot],
            pair_sem.at[wave, slot - row_count],
            recv_sem.at[wave, slot],
            (r, 1 - c),
        )

    def coef_at(plane, place, side_of):
        return coef.at[plane * half + place // 4, :, side_of, place % 4]

    def send_v(place):
        return copy_to(
            v_out.at[place], v_in.at[place], v_send.at[place], v_recv.at[place], (partner, c)
        )

    def send_served(place, j):
        return copy_to(
            served.at[place, j],
            coef_at(1, place, j),
            s_send.at[place, j],
            s_recv.at[place, j],
            (partner, c if j == 0 else 1 - c),
        )

    def send_give(plane, place, index):
        return copy_to(
            give.at[index],
            coef_at(plane, place, 1),
            g_send.at[index],
            g_recv.at[index],
            (r, 1 - c),
        )

    def send_turn(chunk):
        return copy_to(
            u_give.at[chunk],
            u_turn.at[chunk, :, :, pl.ds(4 * rank_rows, 4 * rank_rows)],
            t_send.at[chunk],
            t_recv.at[chunk],
            (r, 1 - c),
        )

    middle = jnp.minimum(z, depth - 1 - z)

    def level_of(step):
        reach = (step + 1) // 2
        near_level = z + jnp.where(step % 2 == 1, reach, -reach)
        beyond = step - middle
        far_level = z + jnp.where(depth - 1 - z > z, beyond, -beyond)
        return jnp.where(step <= 2 * middle, near_level, far_level)

    def tile_at(plane, place):
        level, other = level_of(place // 2), place % 2
        return row_of(level, y + plane - 2 * y * plane, x + other - 2 * x * other)

    def complex_rows(prod, at):
        at = 2 * rank_rows * at
        return combine_parts(prod[at:at + rank_rows], prod[at + rank_rows:at + 2 * rank_rows])

    def project(plane, place, tile, index):
        chunk, at = plane * half + place // 4, place % 4
        for wave in range(waves):
            factors = [
                v_buf[wave, table[0, a, tile]].reshape(2 * rank_rows, -1) for a in (c, 1 - c)
            ]
            prod = jnp.dot(
                jnp.concatenate(factors, axis=0),
                tiles[wave, tile],
                preferred_element_type=jnp.float32,
            )
            coef[chunk, wave, 0, at] = complex_rows(prod, 0).astype(jnp.bfloat16)
            give[index, wave] = complex_rows(prod, 1).astype(jnp.bfloat16)
        send_give(plane, place, index).start()

    def serve(place, tile):
        for wave in range(waves):
            left = v_in[place, wave].reshape(row_blocks * 2 * rank_rows, -1)
            prod = jnp.dot(left, tiles[wave, tile], preferred_element_type=jnp.float32)
            for j in range(row_blocks):
                served[place, j, wave] = complex_rows(prod, j).astype(jnp.bfloat16)
        for j in range(row_blocks):
            send_served(place, j).start()

    def arrive(wave, tile):
        pltpu.make_async_copy(tiles.at[wave, tile], tiles.at[wave, tile], recv_sem.at[wave, tile]).wait()

    def share_edge(wave, tile):
        @pl.when(tile == edge_tile)
        def _():
            to_pair(wave, tile, edge_slot).start()

    for wave in range(waves):
        load_x[wave].wait()
        along_x(wave, r).start()

        @pl.when(has_up)
        def _():
            along_z(wave, r, 1).start()

        @pl.when(has_down)
        def _():
            along_z(wave, r, -1).start()

        to_pair(wave, r, own_slot).start()

    load_v.wait()

    def push_v(place, carry):
        tile = tile_at(1, place)
        for a in range(row_blocks):
            look_up(a, tile)

        @pl.when(tile != corner)
        def _():
            for wave in range(waves):
                for j, a in enumerate((c, 1 - c)):
                    v_out[place, wave, j] = v_buf[wave, table[0, a, tile]]
            send_v(place).start()

        return carry

    lax.fori_loop(0, places, push_v, 0)

    def find_own(place, carry):
        for a in range(row_blocks):
            look_up(a, tile_at(0, place))
        return carry

    lax.fori_loop(0, places, find_own, 0)
    load_u.wait()
    load_near.wait()
    rank_ids = lax.broadcasted_iota(jnp.int32, (rank_rows, tile_rows), 0)

    def place_u(chunk):
        plane, first = chunk // half, (chunk % half) * 4
        for wave in range(waves):
            for j, a in enumerate((c, 1 - c)):
                for part in range(2):
                    rows = []
                    for at in range(4):
                        tile = tile_at(plane, first + at)
                        factor = u_buf[wave, table[0, a, tile], part].astype(jnp.float32)
                        rows.append(jnp.where(rank_ids < table[1, a, tile], factor, 0.0))
                    flipped = jnp.concatenate(rows, axis=0).T.astype(jnp.bfloat16)
                    lines = pl.ds(part * tile_rows, tile_rows)
                    if j == 0:
                        u_turn[chunk, wave, lines, 0:4 * rank_rows] = flipped
                    else:
                        u_give[chunk, wave, lines, :] = flipped
        send_turn(chunk).start()

    def use_tile(place, chunk=None):
        tile = tile_at(0, place)
        project(0, place, tile, place)
        if chunk is not None:
            place_u(chunk)

        @pl.when(tile != partner_corner)
        def _():
            send_v(place).wait_recv()
            serve(place, tile)

    def spread(step, carry):
        @pl.when(step < depth)
        def _():
            level = level_of(step)
            tile = row_of(level, y, x)

            @pl.when(step > 0)
            def _():
                for wave in range(waves):
                    arrive(wave, tile)

                    @pl.when((level < z) & has_up)
                    def _():
                        along_z(wave, tile, 1).start()

                    @pl.when((level > z) & has_down)
                    def _():
                        along_z(wave, tile, -1).start()

                    along_x(wave, tile).start()

            use_tile(2 * step, step)

        @pl.when(step >= 1)
        def _():
            place = 2 * step - 1
            tile = tile_at(0, place)
            for wave in range(waves):
                arrive(wave, tile)
                share_edge(wave, tile)

                @pl.when(tile == partner_corner)
                def _():
                    along_y(wave, tile).start()

            use_tile(place)

        return carry

    lax.fori_loop(0, depth + 1, spread, 0)

    corner_place = 1
    for step in range(depth):
        corner_place += jnp.where(row_of(level_of(step), 1 - y, 1 - x) == corner, 2 * step, 0)
    for wave in range(waves):
        arrive(wave, corner)
        share_edge(wave, corner)
    project(1, corner_place, corner, places)

    def far_chunk(chunk, wave):
        right = coef[chunk, wave].reshape(-1, coef.shape[-1])
        return jnp.dot(u_turn[chunk, wave], right, preferred_element_type=jnp.float32)

    for wave in range(waves):
        arrive(wave, own_slot)
        arrive(wave, edge_slot)
    for chunk in range(half):
        send_turn(chunk).wait_recv()
    for place in range(places):
        send_give(0, place, place).wait_recv()

    def place_of(offset):
        even = (r + offset // 2 + row_count) % row_count
        same_chip = offset == 1 - 2 * c
        return jnp.where(offset % 2 == 0, even, jnp.where(same_chip, own_slot, edge_slot))

    def first_sum(wave, carry):
        value = far_chunk(0, wave)
        for chunk in range(1, half):
            value += far_chunk(chunk, wave)
        for n in range(near_buf.shape[1]):
            left = near_buf[wave, n].reshape(2 * tile_rows, tile_rows)
            block = tiles[wave, place_of(offset_ref[0, n])]
            value += jnp.dot(left, block, preferred_element_type=jnp.float32)
        total[wave] = value
        return carry

    lax.fori_loop(0, waves, first_sum, 0)

    for chunk in range(half):
        send_turn(half + chunk).wait_recv()
        for place in range(4 * chunk, 4 * chunk + 4):
            tile = tile_at(1, place)

            @pl.when(tile != corner)
            def _():
                for j in range(row_blocks):
                    send_served(place, j).wait_recv()

            @pl.when(tile == corner)
            def _():
                send_give(1, place, places).wait_recv()

        for wave in range(waves):
            value = total[wave] + far_chunk(half + chunk, wave)
            if chunk < half - 1:
                total[wave] = value
            else:
                out_ref[wave] = combine_parts(value[:tile_rows], value[tile_rows:]).astype(out_ref.dtype)

    for wave in range(waves):
        to_pair(wave, r, own_slot).wait_send()
        to_pair(wave, edge_tile, edge_slot).wait_send()
        along_y(wave, partner_corner).wait_send()
    send_give(1, corner_place, places).wait_send()

    def drain(step, carry):
        level = level_of(step)
        tile = row_of(level, y, x)
        send_turn(step).wait_send()
        for wave in range(waves):
            along_x(wave, tile).wait_send()

            @pl.when((level <= z) & has_up)
            def _():
                along_z(wave, tile, 1).wait_send()

            @pl.when((level >= z) & has_down)
            def _():
                along_z(wave, tile, -1).wait_send()

        for other in range(2):
            place = 2 * step + other
            send_give(0, place, place).wait_send()

            @pl.when(tile_at(1, place) != corner)
            def _():
                send_v(place).wait_send()

            @pl.when(tile_at(0, place) != partner_corner)
            def _():
                for j in range(row_blocks):
                    send_served(place, j).wait_send()

        return carry

    lax.fori_loop(0, depth, drain, 0)


def fused_shards(incident, near_tiles, near_offsets, far_row, far_col, far_rank, far_count, far_u, far_v):
    waves, tile_rows, columns = incident.shape
    row_count, row_blocks = lax.axis_size("row"), lax.axis_size("col")
    slots, rank_rows = far_u.shape[3], far_u.shape[5]
    near_slots = near_tiles.shape[2]
    depth, places = row_count // 4, row_count // 2
    bf16, f32 = jnp.bfloat16, jnp.float32
    any_space = pl.BlockSpec(memory_space=pl.ANY)
    smem = pl.BlockSpec(memory_space=pltpu.SMEM)
    vmem = pl.BlockSpec(memory_space=pltpu.VMEM)
    dma = pltpu.SemaphoreType.DMA
    return pl.pallas_call(
        functools.partial(fused_kernel, depth),
        out_shape=jax.ShapeDtypeStruct(incident.shape, bf16),
        in_specs=[smem] * 5 + [any_space] * 4,
        out_specs=vmem,
        scratch_shapes=[
            pltpu.VMEM((waves, row_count + 2, tile_rows, columns), bf16),
            pltpu.VMEM((waves, near_slots, 2, tile_rows, tile_rows), bf16),
            pltpu.VMEM((waves, slots, 2, rank_rows, tile_rows), bf16),
            pltpu.VMEM((waves, slots, 2, rank_rows, tile_rows), bf16),
            pltpu.VMEM((depth, waves, 2 * tile_rows, 8 * rank_rows), bf16),
            pltpu.VMEM((depth, waves, 2 * tile_rows, 4 * rank_rows), bf16),
            pltpu.VMEM((depth, waves, row_blocks, 4, rank_rows, columns), bf16),
            pltpu.VMEM((places + 1, waves, rank_rows, columns), bf16),
            pltpu.VMEM((places, waves, row_blocks, 2, rank_rows, tile_rows), bf16),
            pltpu.VMEM((places, waves, row_blocks, 2, rank_rows, tile_rows), bf16),
            pltpu.VMEM((places, row_blocks, waves, rank_rows, columns), bf16),
            pltpu.VMEM((waves, 2 * tile_rows, columns), f32),
            pltpu.SMEM((slots,), jnp.int32),
            pltpu.SMEM((2, row_blocks, row_count), jnp.int32),
            dma((waves, row_count + 2)),
            dma((waves, row_count, 4)),
            dma((waves, 2)),
            dma((places,)),
            dma((places,)),
            dma((places, row_blocks)),
            dma((places, row_blocks)),
            dma((places + 1,)),
            dma((places + 1,)),
            dma((depth,)),
            dma((depth,)),
            dma((3 + waves,)),
        ],
        compiler_params=pltpu.CompilerParams(collective_id=0, has_side_effects=True),
    )(near_offsets, far_row, far_col, far_rank, far_count, incident, near_tiles, far_u, far_v)


def solution(mesh):
    in_specs = (
        P(None, ("row", "col"), None),
        P(("row", "col"), None, None, None, None, None),
        P(("row", "col"), None),
        P("row", "col", None),
        P("row", "col", None),
        P("row", "col", None),
        P("row", "col"),
        P("row", "col", None, None, None, None, None),
        P("row", "col", None, None, None, None, None),
    )
    out_specs = P(None, ("row", "col"), None)
    paired = mesh.shape["col"] == 2 and mesh.shape["row"] % 8 == 0
    shards = fused_shards if paired else generic_shards
    return jax.shard_map(shards, mesh=mesh, in_specs=in_specs, out_specs=out_specs, check_vma=False)
```

time: 74 us -> 68.8 us (0.930); the launches traced: 73.8 us -> 67.8 us
  Pallas kernels: 69.1 us -> 65.3 us
  other arithmetic: 1.51 us -> 0 us
    pallas_call x1, Pallas kernels: 69.1 us -> 65.3 us  [fused_shards(): pl.pallas_call(functools.partial(fused_kernel, depth), out_shape=jax.Shap...]
where the time goes in v1:
time: 68.8 us; the launch traced here: 67.8 us
  Pallas kernels  65.3 us (95%)
  local copies, waits for them, and re-layouts  1.87 us (3%)
    pallas_call x1, Pallas kernels, fused_shards(): pl.pallas_call(functools.partial(fused_kernel, depth), out_shape=jax.Shap...  65.3 us
    unnamed x1, local copies, waits for them, and re-layouts  1.87 us

profile of v1, /device:TPU:0, one launch (start us, length us, event | category | flops | bytes accessed | tf_op | source)
XLA Modules:
  0.0 67.8 jit_solution(18325089258383575278)
XLA Ops:
  0.7 65.3 %shard_map.91 = bf16[2,256,512]{2,1,0:T(8,128)(2,1)} custom-call(s32[1,3]{1,0:T(1,128)} %offset_ref.1, s32[1,1,16]{2,1,0:T(1,128)} %row_ref.1, s32[1,1,16]{2,1,0:T(1,128)} %col_ref.1, s32[1,1,16]{2,1,0:T(1,128)} %rank_ref.1, s32[1,1]{1,0:T(1,128)S(6)} %copy.11.count_ref, bf16[2,256,512]{2,1,0:T(8,128)(2,1)} %x_hbm.1, ...), custom_call_target="tpu_custom_call" | custom-call | tf_op jit(solution)/shard_map/pallas_call | solution.py:539
  66.0 1.9 %copy.12 = bf16[2,256,512]{2,1,0:T(8,128)(2,1)} copy(bf16[2,256,512]{2,1,0:T(8,128)(2,1)} %shard_map.91) | data formatting | bytes 1048576

commit v2 on v1

--- a/solution.py
+++ b/solution.py
@@ -8,6 +8,7 @@
 from jax.sharding import PartitionSpec as P
 
 MESH = pl.DeviceIdType.MESH
+SIDE_FROM = 0
 UP, DOWN, ALONG_Y, ALONG_X = range(4)
 
 
@@ -131,9 +132,9 @@
 
 
 def fused_kernel(
-    depth, offset_ref, row_ref, col_ref, rank_ref, count_ref, x_hbm, near_hbm, u_hbm, v_hbm, out_ref,
-    tiles, near_buf, u_buf, v_buf, u_turn, u_give, coef, give, v_out, v_in, served, total, keys, table,
-    recv_sem, send_sem, pair_sem, v_send, v_recv, s_send, s_recv, g_send, g_recv, t_send, t_recv, load_sem,
+    depth, offset_ref, row_ref, col_ref, rank_ref, count_ref, x_hbm, near_hbm, u_hbm, v_hbm, out_hbm,
+    tiles, close, near_buf, u_buf, v_buf, u_turn, u_give, coef, give, v_out, v_in, served, total, out_buf, keys, table,
+    recv_sem, send_sem, pair_sem, v_send, v_recv, s_send, s_recv, g_send, g_recv, t_send, t_recv, load_sem, out_sem,
 ):
     waves = tiles.shape[0]
     row_count = depth * 4
@@ -148,11 +149,28 @@
     z, y, x = r // 4, (r // 2) % 2, r % 2
     own_slot, edge_slot = row_count, row_count + 1
     edge_tile = (r + 1 - 2 * c + row_count) % row_count
-    side = 2 * x - 1
     partner = r + 2 * (1 - 2 * y)
-    corner = (r + side + row_count) % row_count
-    partner_corner = (partner + side + row_count) % row_count
     has_up, has_down = z < depth - 1, z > 0
+    beside = r + 1 - 2 * x
+    low_end, high_end = 2, row_count - 3
+    doubled = c == 1
+    is_end = ((r == low_end) | (r == high_end)) & ~doubled
+    is_feeder = ((beside == low_end) | (beside == high_end)) & ~doubled
+    across = partner + 1 - 2 * x
+
+    def corner_of(row):
+        return (row + 2 * (row % 2) - 1 + row_count) % row_count
+
+    def at_wrap(row):
+        return (row == 0) | (row == row_count - 1)
+
+    leaps = doubled & at_wrap(across)
+    leapt = doubled & at_wrap(r)
+
+    def serves_side(row):
+        return (c >= SIDE_FROM) & ~at_wrap(row)
+
+    corner, partner_corner = corner_of(r), corner_of(partner)
 
     def row_of(tz, ty, tx):
         return (tz * 2 + ty) * 2 + tx
@@ -172,8 +190,12 @@
     def greet(device):
         pl.semaphore_signal(barrier, inc=1, device_id=device, device_id_type=MESH)
 
-    for device in ((partner, c), (partner, 1 - c), (row_of(z, y, 1 - x), c), (r, 1 - c)):
+    for device in ((partner, c), (partner, 1 - c), (beside, c), (beside, 1 - c), (r, 1 - c)):
         greet(device)
+
+    @pl.when(leapt)
+    def _():
+        greet((across, c))
 
     @pl.when(has_up)
     def _():
@@ -197,7 +219,7 @@
         table[0, a, tile] = slot
         table[1, a, tile] = rank
 
-    pl.semaphore_wait(barrier, 4 + jnp.where(has_up, 1, 0) + jnp.where(has_down, 1, 0))
+    pl.semaphore_wait(barrier, 5 + jnp.where(has_up, 1, 0) + jnp.where(has_down, 1, 0) + jnp.where(leaps, 1, 0))
 
     def copy_to(source, target, sent, received, device):
         return pltpu.make_async_remote_copy(
@@ -211,49 +233,63 @@
 
     def hop(wave, tile, link, row):
         here = tiles.at[wave, tile]
-        return copy_to(here, here, send_sem.at[wave, tile, link], recv_sem.at[wave, tile], (row, c))
+        return copy_to(here, here, send_sem.at[link], recv_sem.at[wave, tile], (row, c))
 
     def along_z(wave, tile, step):
         return hop(wave, tile, (1 - step) // 2, row_of(z + step, y, x))
 
     def along_x(wave, tile):
-        return hop(wave, tile, ALONG_X, row_of(z, y, 1 - x))
+        return hop(wave, tile, ALONG_X, beside)
 
     def along_y(wave, tile):
         return hop(wave, tile, ALONG_Y, partner)
+
+    def leap(wave):
+        return hop(wave, corner_of(across), ALONG_Y, across)
 
     def to_pair(wave, tile, slot):
         return copy_to(
             tiles.at[wave, tile],
-            tiles.at[wave, slot],
-            pair_sem.at[wave, slot - row_count],
+            close.at[wave, slot - row_count + 2],
+            pair_sem.at[0],
             recv_sem.at[wave, slot],
             (r, 1 - c),
         )
 
-    def coef_at(plane, place, side_of):
-        return coef.at[plane * half + place // 4, :, side_of, place % 4]
-
     def send_v(place):
         return copy_to(
-            v_out.at[place], v_in.at[place], v_send.at[place], v_recv.at[place], (partner, c)
-        )
-
-    def send_served(place, j):
+            v_out.at[place], v_in.at[place], v_send.at[0], v_recv.at[place], (partner, c)
+        )
+
+    def send_v_side(place):
         return copy_to(
-            served.at[place, j],
-            coef_at(1, place, j),
-            s_send.at[place, j],
-            s_recv.at[place, j],
+            v_out.at[place], v_in.at[places], v_send.at[0], v_recv.at[places], (beside, c)
+        )
+
+    def send_served(place, wave, j):
+        return copy_to(
+            served.at[place, wave, j],
+            coef.at[half + place // 4, wave, j, place % 4],
+            s_send.at[0],
+            s_recv.at[place // 4],
             (partner, c if j == 0 else 1 - c),
+        )
+
+    def send_served_side(place, wave, j):
+        return copy_to(
+            served.at[places, wave, j],
+            coef.at[half + place // 4, wave, j, place % 4],
+            s_send.at[0],
+            s_recv.at[place // 4],
+            (beside, c if j == 0 else 1 - c),
         )
 
     def send_give(plane, place, index):
         return copy_to(
             give.at[index],
-            coef_at(plane, place, 1),
-            g_send.at[index],
-            g_recv.at[index],
+            coef.at[plane * half + place // 4, :, 1, place % 4],
+            g_send.at[0],
+            g_recv.at[half if plane else place // 4],
             (r, 1 - c),
         )
 
@@ -261,7 +297,7 @@
         return copy_to(
             u_give.at[chunk],
             u_turn.at[chunk, :, :, pl.ds(4 * rank_rows, 4 * rank_rows)],
-            t_send.at[chunk],
+            t_send.at[0],
             t_recv.at[chunk],
             (r, 1 - c),
         )
@@ -283,32 +319,30 @@
         at = 2 * rank_rows * at
         return combine_parts(prod[at:at + rank_rows], prod[at + rank_rows:at + 2 * rank_rows])
 
-    def project(plane, place, tile, index):
-        chunk, at = plane * half + place // 4, place % 4
-        for wave in range(waves):
-            factors = [
-                v_buf[wave, table[0, a, tile]].reshape(2 * rank_rows, -1) for a in (c, 1 - c)
-            ]
-            prod = jnp.dot(
-                jnp.concatenate(factors, axis=0),
-                tiles[wave, tile],
-                preferred_element_type=jnp.float32,
-            )
-            coef[chunk, wave, 0, at] = complex_rows(prod, 0).astype(jnp.bfloat16)
-            give[index, wave] = complex_rows(prod, 1).astype(jnp.bfloat16)
-        send_give(plane, place, index).start()
-
-    def serve(place, tile):
-        for wave in range(waves):
-            left = v_in[place, wave].reshape(row_blocks * 2 * rank_rows, -1)
-            prod = jnp.dot(left, tiles[wave, tile], preferred_element_type=jnp.float32)
-            for j in range(row_blocks):
-                served[place, j, wave] = complex_rows(prod, j).astype(jnp.bfloat16)
+    def project(plane, place, tile, index, wave):
+        factors = [v_buf[wave, table[0, a, tile]].reshape(2 * rank_rows, -1) for a in (c, 1 - c)]
+        prod = jnp.dot(
+            jnp.concatenate(factors, axis=0), tiles[wave, tile], preferred_element_type=jnp.float32
+        )
+        chunk = plane * half + place // 4
+        coef[chunk, wave, 0, place % 4] = complex_rows(prod, 0).astype(jnp.bfloat16)
+        give[index, wave] = complex_rows(prod, 1).astype(jnp.bfloat16)
+        if wave == waves - 1:
+            send_give(plane, place, index).start()
+
+    def serve(place, tile, wave, send):
+        left = v_in[place, wave].reshape(row_blocks * 2 * rank_rows, -1)
+        prod = jnp.dot(left, tiles[wave, tile], preferred_element_type=jnp.float32)
         for j in range(row_blocks):
-            send_served(place, j).start()
+            served[place, wave, j] = complex_rows(prod, j).astype(jnp.bfloat16)
+        for j in range(row_blocks):
+            send(wave, j).start()
+
+    def await_bytes(part, sem):
+        pltpu.make_async_copy(part, part, sem).wait()
 
     def arrive(wave, tile):
-        pltpu.make_async_copy(tiles.at[wave, tile], tiles.at[wave, tile], recv_sem.at[wave, tile]).wait()
+        await_bytes(tiles.at[wave, r], recv_sem.at[wave, tile])
 
     def share_edge(wave, tile):
         @pl.when(tile == edge_tile)
@@ -341,7 +375,15 @@
             for wave in range(waves):
                 for j, a in enumerate((c, 1 - c)):
                     v_out[place, wave, j] = v_buf[wave, table[0, a, tile]]
-            send_v(place).start()
+            aside = (tile == corner_of(beside)) & serves_side(beside)
+
+            @pl.when(aside)
+            def _():
+                send_v_side(place).start()
+
+            @pl.when(~aside)
+            def _():
+                send_v(place).start()
 
         return carry
 
@@ -375,154 +417,261 @@
                         u_give[chunk, wave, lines, :] = flipped
         send_turn(chunk).start()
 
-    def use_tile(place, chunk=None):
+    def served_here(tile):
+        return (tile != partner_corner) & ~((tile == corner_of(across)) & serves_side(across))
+
+    def use_tile(place, tile, wave):
+        @pl.when(served_here(tile))
+        def _():
+            if wave == 0:
+                send_v(place).wait_recv()
+            serve(place, tile, wave, functools.partial(send_served, place))
+
+        project(0, place, tile, place, wave)
+
+    def at_end(level):
+        return (level == 0) | (level == depth - 1)
+
+    def forward(step, tile, wave):
+        level = level_of(step)
+        arrive(wave, tile)
+
+        @pl.when(leaps & (tile == corner_of(across)))
+        def _():
+            leap(wave).start()
+
+        @pl.when((level < z) & has_up)
+        def _():
+            along_z(wave, tile, 1).start()
+
+        @pl.when((level > z) & has_down)
+        def _():
+            along_z(wave, tile, -1).start()
+
+        held = wave == waves - 1
+
+        crosses = ~(is_feeder & (step == depth - 2)) if held else step > 0
+
+        @pl.when(crosses & ~(doubled & at_end(level)))
+        def _():
+            along_x(wave, tile).start()
+
+        if held:
+            @pl.when(is_feeder & (step == depth - 1))
+            def _():
+                along_x(wave, tile_at(0, 2 * step - 2)).start()
+
+    def take_side(place, wave):
         tile = tile_at(0, place)
-        project(0, place, tile, place)
-        if chunk is not None:
-            place_u(chunk)
-
-        @pl.when(tile != partner_corner)
-        def _():
-            send_v(place).wait_recv()
-            serve(place, tile)
-
-    def spread(step, carry):
-        @pl.when(step < depth)
-        def _():
-            level = level_of(step)
-            tile = row_of(level, y, x)
-
-            @pl.when(step > 0)
-            def _():
-                for wave in range(waves):
-                    arrive(wave, tile)
-
-                    @pl.when((level < z) & has_up)
-                    def _():
-                        along_z(wave, tile, 1).start()
-
-                    @pl.when((level > z) & has_down)
-                    def _():
-                        along_z(wave, tile, -1).start()
-
-                    along_x(wave, tile).start()
-
-            use_tile(2 * step, step)
-
-        @pl.when(step >= 1)
-        def _():
-            place = 2 * step - 1
-            tile = tile_at(0, place)
-            for wave in range(waves):
-                arrive(wave, tile)
-                share_edge(wave, tile)
-
-                @pl.when(tile == partner_corner)
-                def _():
-                    along_y(wave, tile).start()
-
-            use_tile(place)
-
-        return carry
-
-    lax.fori_loop(0, depth + 1, spread, 0)
+        arrive(wave, tile)
+        share_edge(wave, tile)
+        level = level_of(place // 2)
+        passes = doubled & at_end(level)
+
+        @pl.when(passes & (level <= z) & has_up)
+        def _():
+            along_z(wave, tile, 1).start()
+
+        @pl.when(passes & (level >= z) & has_down)
+        def _():
+            along_z(wave, tile, -1).start()
+
+        @pl.when((tile == partner_corner) & ~(doubled & at_wrap(partner)))
+        def _():
+            along_y(wave, tile).start()
 
     corner_place = 1
     for step in range(depth):
         corner_place += jnp.where(row_of(level_of(step), 1 - y, 1 - x) == corner, 2 * step, 0)
-    for wave in range(waves):
-        arrive(wave, corner)
-        share_edge(wave, corner)
-    project(1, corner_place, corner, places)
+
+    def use_corner():
+        for wave in range(waves):
+            arrive(wave, corner)
+            share_edge(wave, corner)
+
+            @pl.when(serves_side(r))
+            def _():
+                if wave == 0:
+                    send_v_side(0).wait_recv()
+                serve(places, corner, wave, functools.partial(send_served_side, corner_place - 1))
+
+            project(1, corner_place, corner, places, wave)
 
     def far_chunk(chunk, wave):
         right = coef[chunk, wave].reshape(-1, coef.shape[-1])
         return jnp.dot(u_turn[chunk, wave], right, preferred_element_type=jnp.float32)
 
-    for wave in range(waves):
-        arrive(wave, own_slot)
-        arrive(wave, edge_slot)
-    for chunk in range(half):
-        send_turn(chunk).wait_recv()
-    for place in range(places):
-        send_give(0, place, place).wait_recv()
-
     def place_of(offset):
-        even = (r + offset // 2 + row_count) % row_count
-        same_chip = offset == 1 - 2 * c
-        return jnp.where(offset % 2 == 0, even, jnp.where(same_chip, own_slot, edge_slot))
-
-    def first_sum(wave, carry):
-        value = far_chunk(0, wave)
-        for chunk in range(1, half):
-            value += far_chunk(chunk, wave)
+        across_chip = jnp.where(offset == 1 - 2 * c, 2, 3)
+        return jnp.where(offset % 2 == 0, jnp.where(offset == 2 * (beside - r), 0, 1), across_chip)
+
+    def near_sum(wave):
+        value = None
         for n in range(near_buf.shape[1]):
             left = near_buf[wave, n].reshape(2 * tile_rows, tile_rows)
-            block = tiles[wave, place_of(offset_ref[0, n])]
-            value += jnp.dot(left, block, preferred_element_type=jnp.float32)
+            block = close[wave, place_of(offset_ref[0, n])] if n else tiles[wave, r]
+            prod = jnp.dot(left, block, preferred_element_type=jnp.float32)
+            value = prod if value is None else value + prod
+        return value
+
+    def await_chunk(chunk):
+        await_bytes(u_give.at[0], t_recv.at[chunk])
+        part = coef.at[chunk]
+        if chunk < half:
+            await_bytes(part.at[:, 1], g_recv.at[chunk])
+        else:
+            sem = s_recv.at[chunk - half]
+            holds_corner = corner_place // 4 == chunk - half
+
+            @pl.when(holds_corner)
+            def _():
+                await_bytes(part.at[:, :, 0:3], sem)
+                await_bytes(give.at[0], g_recv.at[half])
+
+            @pl.when(~holds_corner)
+            def _():
+                await_bytes(part, sem)
+
+    def add_chunk(chunk):
+        await_chunk(chunk)
+        for wave in range(waves):
+            total[wave] += far_chunk(chunk, wave)
+
+    def await_near():
+        for wave in range(waves):
+            arrive(wave, own_slot)
+            arrive(wave, edge_slot)
+            close[wave, 0] = tiles[wave, beside]
+            close[wave, 1] = tiles[wave, corner]
+
+    def await_first():
+        for chunk in range(half - 1):
+            await_chunk(chunk)
+
+    def first_sum(with_near, wave, carry):
+        value = near_sum(wave) if with_near else jnp.zeros(total.shape[1:], jnp.float32)
+        for chunk in range(half - 1):
+            value += far_chunk(chunk, wave)
         total[wave] = value
         return carry
 
-    lax.fori_loop(0, waves, first_sum, 0)
-
-    for chunk in range(half):
-        send_turn(half + chunk).wait_recv()
-        for place in range(4 * chunk, 4 * chunk + 4):
-            tile = tile_at(1, place)
-
-            @pl.when(tile != corner)
+    def add_near(wave, carry):
+        total[wave] += near_sum(wave)
+        return carry
+
+    def put_out(wave):
+        return pltpu.make_async_copy(out_buf.at[wave], out_hbm.at[wave], out_sem.at[wave])
+
+    def comes_early(step):
+        return doubled & has_up & has_down & at_end(level_of(step))
+
+    def spread(distance, carry):
+        behind = 2 * distance - 1
+
+        @pl.when(distance < depth)
+        def _():
+            place_u(distance)
+
+        @pl.when(distance == 0)
+        def _():
+            for wave in range(waves):
+                use_tile(0, r, wave)
+
+        @pl.when((distance == depth) & ~at_wrap(r))
+        def _():
+            use_corner()
+            await_near()
+            await_first()
+            lax.fori_loop(0, waves, functools.partial(first_sum, True), 0)
+
+        @pl.when(distance > 0)
+        def _():
+            for wave in range(waves):
+                for sign in (1, -1):
+                    level = z + sign * distance
+
+                    @pl.when((level >= 0) & (level < depth))
+                    def _():
+                        first = 2 * distance - (1 if sign == 1 else 0)
+                        step = jnp.where(distance <= middle, first, middle + distance)
+                        tile = row_of(level, y, x)
+                        forward(step, tile, wave)
+                        use_tile(2 * step, tile, wave)
+
+                if wave == waves - 1:
+                    @pl.when(is_end & (distance == depth - 1))
+                    def _():
+                        for early in range(waves):
+                            take_side(places - 1, early)
+
+                @pl.when(~comes_early(distance - 1))
+                def _():
+                    @pl.when(~(is_end & (distance == depth)))
+                    def _():
+                        take_side(behind, wave)
+
+                    use_tile(behind, tile_at(0, behind), wave)
+
+                @pl.when(comes_early(distance) & (distance < depth))
+                def _():
+                    take_side(behind + 2, wave)
+                    use_tile(behind + 2, tile_at(0, behind + 2), wave)
+
+        return carry
+
+    lax.fori_loop(0, depth + 1, spread, 0)
+
+    @pl.when(at_wrap(r))
+    def _():
+        await_first()
+        lax.fori_loop(0, waves, functools.partial(first_sum, False), 0)
+
+    add_chunk(half - 1)
+    for chunk in range(half, depth - 1):
+        add_chunk(chunk)
+
+    @pl.when(at_wrap(r))
+    def _():
+        use_corner()
+        await_near()
+        lax.fori_loop(0, waves, add_near, 0)
+
+    await_chunk(depth - 1)
+    for wave in range(waves):
+        value = total[wave] + far_chunk(depth - 1, wave)
+        out_buf[wave] = combine_parts(value[:tile_rows], value[tile_rows:]).astype(out_buf.dtype)
+        put_out(wave).start()
+
+    def await_count(parts, count, most, sem):
+        for n in range(1, most + 1):
+            @pl.when(count == n)
             def _():
-                for j in range(row_blocks):
-                    send_served(place, j).wait_recv()
-
-            @pl.when(tile == corner)
-            def _():
-                send_give(1, place, places).wait_recv()
-
-        for wave in range(waves):
-            value = total[wave] + far_chunk(half + chunk, wave)
-            if chunk < half - 1:
-                total[wave] = value
-            else:
-                out_ref[wave] = combine_parts(value[:tile_rows], value[tile_rows:]).astype(out_ref.dtype)
-
+                await_bytes(parts(n), sem)
+
+    def one_if(flag):
+        return jnp.where(flag, 1, 0)
+
+    def some_tiles(n):
+        return tiles.at[:, 0:n]
+
+    def ends_but(level):
+        return one_if(doubled) * (2 - one_if(at_end(level)))
+
+    await_bytes(some_tiles(2), pair_sem.at[0])
+    await_bytes(v_out.at[0:places - 1], v_send.at[0])
+    await_bytes(give, g_send.at[0])
+    await_bytes(u_give, t_send.at[0])
+    sides = places - 1 - one_if(serves_side(across)) + one_if(serves_side(r))
+    await_count(lambda n: served.at[0:n], sides, places, s_send.at[0])
+    ups = one_if(has_up) * (z + 1 + one_if(doubled))
+    await_count(some_tiles, ups, depth, send_sem.at[UP])
+    downs = one_if(has_down) * (depth - z + one_if(doubled))
+    await_count(some_tiles, downs, depth, send_sem.at[DOWN])
+    await_count(some_tiles, depth - ends_but(z), depth, send_sem.at[ALONG_X])
+    lines = one_if(leaps) + one_if(~(doubled & at_wrap(partner)))
+    await_count(some_tiles, lines, 2, send_sem.at[ALONG_Y])
     for wave in range(waves):
-        to_pair(wave, r, own_slot).wait_send()
-        to_pair(wave, edge_tile, edge_slot).wait_send()
-        along_y(wave, partner_corner).wait_send()
-    send_give(1, corner_place, places).wait_send()
-
-    def drain(step, carry):
-        level = level_of(step)
-        tile = row_of(level, y, x)
-        send_turn(step).wait_send()
-        for wave in range(waves):
-            along_x(wave, tile).wait_send()
-
-            @pl.when((level <= z) & has_up)
-            def _():
-                along_z(wave, tile, 1).wait_send()
-
-            @pl.when((level >= z) & has_down)
-            def _():
-                along_z(wave, tile, -1).wait_send()
-
-        for other in range(2):
-            place = 2 * step + other
-            send_give(0, place, place).wait_send()
-
-            @pl.when(tile_at(1, place) != corner)
-            def _():
-                send_v(place).wait_send()
-
-            @pl.when(tile_at(0, place) != partner_corner)
-            def _():
-                for j in range(row_blocks):
-                    send_served(place, j).wait_send()
-
-        return carry
-
-    lax.fori_loop(0, depth, drain, 0)
+        put_out(wave).wait()
 
 
 def fused_shards(incident, near_tiles, near_offsets, far_row, far_col, far_rank, far_count, far_u, far_v):
@@ -530,19 +679,19 @@
     row_count, row_blocks = lax.axis_size("row"), lax.axis_size("col")
     slots, rank_rows = far_u.shape[3], far_u.shape[5]
     near_slots = near_tiles.shape[2]
-    depth, places = row_count // 4, row_count // 2
+    depth, places, half = row_count // 4, row_count // 2, row_count // 8
     bf16, f32 = jnp.bfloat16, jnp.float32
     any_space = pl.BlockSpec(memory_space=pl.ANY)
     smem = pl.BlockSpec(memory_space=pltpu.SMEM)
-    vmem = pl.BlockSpec(memory_space=pltpu.VMEM)
     dma = pltpu.SemaphoreType.DMA
     return pl.pallas_call(
         functools.partial(fused_kernel, depth),
         out_shape=jax.ShapeDtypeStruct(incident.shape, bf16),
         in_specs=[smem] * 5 + [any_space] * 4,
-        out_specs=vmem,
+        out_specs=any_space,
         scratch_shapes=[
-            pltpu.VMEM((waves, row_count + 2, tile_rows, columns), bf16),
+            pltpu.VMEM((waves, row_count, tile_rows, columns), bf16),
+            pltpu.VMEM((waves, 4, tile_rows, columns), bf16),
             pltpu.VMEM((waves, near_slots, 2, tile_rows, tile_rows), bf16),
             pltpu.VMEM((waves, slots, 2, rank_rows, tile_rows), bf16),
             pltpu.VMEM((waves, slots, 2, rank_rows, tile_rows), bf16),
@@ -551,23 +700,25 @@
             pltpu.VMEM((depth, waves, row_blocks, 4, rank_rows, columns), bf16),
             pltpu.VMEM((places + 1, waves, rank_rows, columns), bf16),
             pltpu.VMEM((places, waves, row_blocks, 2, rank_rows, tile_rows), bf16),
-            pltpu.VMEM((places, waves, row_blocks, 2, rank_rows, tile_rows), bf16),
-            pltpu.VMEM((places, row_blocks, waves, rank_rows, columns), bf16),
+            pltpu.VMEM((places + 1, waves, row_blocks, 2, rank_rows, tile_rows), bf16),
+            pltpu.VMEM((places + 1, waves, row_blocks, rank_rows, columns), bf16),
             pltpu.VMEM((waves, 2 * tile_rows, columns), f32),
+            pltpu.VMEM(incident.shape, bf16),
             pltpu.SMEM((slots,), jnp.int32),
             pltpu.SMEM((2, row_blocks, row_count), jnp.int32),
             dma((waves, row_count + 2)),
-            dma((waves, row_count, 4)),
-            dma((waves, 2)),
-            dma((places,)),
-            dma((places,)),
-            dma((places, row_blocks)),
-            dma((places, row_blocks)),
+            dma((4,)),
+            dma((1,)),
+            dma((1,)),
             dma((places + 1,)),
-            dma((places + 1,)),
-            dma((depth,)),
+            dma((1,)),
+            dma((half,)),
+            dma((1,)),
+            dma((half + 1,)),
+            dma((1,)),
             dma((depth,)),
             dma((3 + waves,)),
+            dma((waves,)),
         ],
         compiler_params=pltpu.CompilerParams(collective_id=0, has_side_effects=True),
     )(near_offsets, far_row, far_col, far_rank, far_count, incident, near_tiles, far_u, far_v)

time: 68.8 us -> 63.1 us (0.917)
  Pallas kernels: 65.3 us -> 60.1 us
    pallas_call x1, Pallas kernels: 65.3 us -> 60.1 us  [fused_shards(): pl.pallas_call(functools.partial(fused_kernel, depth), out_shape=jax.Shap...]
where the time goes in v2:
time: 63.1 us; the launch traced here: 62.6 us
  Pallas kernels  60.1 us (95%)
  local copies, waits for them, and re-layouts  1.87 us (3%)
  between operations  0.66 us (1%)
    pallas_call x1, Pallas kernels, fused_shards(): pl.pallas_call(functools.partial(fused_kernel, depth), out_shape=jax.Shap...  60.1 us
    unnamed x1, local copies, waits for them, and re-layouts  1.87 us

profile of v2, /device:TPU:0, one launch (start us, length us, event | category | flops | bytes accessed | tf_op | source)
XLA Modules:
  0.0 62.6 jit_solution(16855636784313302087)
XLA Ops:
  0.7 60.1 %shard_map.91 = bf16[2,256,512]{2,1,0:T(8,128)(2,1)} custom-call(s32[1,3]{1,0:T(1,128)} %offset_ref.1, s32[1,1,16]{2,1,0:T(1,128)} %row_ref.1, s32[1,1,16]{2,1,0:T(1,128)} %col_ref.1, s32[1,1,16]{2,1,0:T(1,128)} %rank_ref.1, s32[1,1]{1,0:T(1,128)S(6)} %copy.11.count_ref, bf16[2,256,512]{2,1,0:T(8,128)(2,1)} %x_hbm.1, ...), custom_call_target="tpu_custom_call" | custom-call | tf_op jit(solution)/shard_map/pallas_call | solution.py:687
  60.7 1.9 %copy.12 = bf16[2,256,512]{2,1,0:T(8,128)(2,1)} copy(bf16[2,256,512]{2,1,0:T(8,128)(2,1)} %shard_map.91) | data formatting | bytes 1048576

commit v3 on v2

--- a/solution.py
+++ b/solution.py
@@ -8,7 +8,6 @@
 from jax.sharding import PartitionSpec as P
 
 MESH = pl.DeviceIdType.MESH
-SIDE_FROM = 0
 UP, DOWN, ALONG_Y, ALONG_X = range(4)
 
 
@@ -132,9 +131,9 @@
 
 
 def fused_kernel(
-    depth, offset_ref, row_ref, col_ref, rank_ref, count_ref, x_hbm, near_hbm, u_hbm, v_hbm, out_hbm,
-    tiles, close, near_buf, u_buf, v_buf, u_turn, u_give, coef, give, v_out, v_in, served, total, out_buf, keys, table,
-    recv_sem, send_sem, pair_sem, v_send, v_recv, s_send, s_recv, g_send, g_recv, t_send, t_recv, load_sem, out_sem,
+    depth, offset_ref, row_ref, col_ref, rank_ref, count_ref, x_hbm, near_hbm, u_hbm, v_hbm, out_ref,
+    tiles, close, near_buf, u_buf, v_buf, u_turn, u_give, coef, give, v_out, v_in, served, total, keys, table,
+    recv_sem, send_sem, pair_sem, v_send, v_recv, s_send, s_recv, g_send, g_recv, t_send, t_recv, load_sem,
 ):
     waves = tiles.shape[0]
     row_count = depth * 4
@@ -168,7 +167,8 @@
     leapt = doubled & at_wrap(r)
 
     def serves_side(row):
-        return (c >= SIDE_FROM) & ~at_wrap(row)
+        from_end = jnp.minimum(row, row_count - 1 - row)
+        return (from_end == 1) | (from_end > 3)
 
     corner, partner_corner = corner_of(r), corner_of(partner)
 
@@ -559,9 +559,6 @@
         total[wave] += near_sum(wave)
         return carry
 
-    def put_out(wave):
-        return pltpu.make_async_copy(out_buf.at[wave], out_hbm.at[wave], out_sem.at[wave])
-
     def comes_early(step):
         return doubled & has_up & has_down & at_end(level_of(step))
 
@@ -639,8 +636,7 @@
     await_chunk(depth - 1)
     for wave in range(waves):
         value = total[wave] + far_chunk(depth - 1, wave)
-        out_buf[wave] = combine_parts(value[:tile_rows], value[tile_rows:]).astype(out_buf.dtype)
-        put_out(wave).start()
+        out_ref[wave] = combine_parts(value[:tile_rows], value[tile_rows:]).astype(out_ref.dtype)
 
     def await_count(parts, count, most, sem):
         for n in range(1, most + 1):
@@ -670,8 +666,6 @@
     await_count(some_tiles, depth - ends_but(z), depth, send_sem.at[ALONG_X])
     lines = one_if(leaps) + one_if(~(doubled & at_wrap(partner)))
     await_count(some_tiles, lines, 2, send_sem.at[ALONG_Y])
-    for wave in range(waves):
-        put_out(wave).wait()
 
 
 def fused_shards(incident, near_tiles, near_offsets, far_row, far_col, far_rank, far_count, far_u, far_v):
@@ -686,9 +680,9 @@
     dma = pltpu.SemaphoreType.DMA
     return pl.pallas_call(
         functools.partial(fused_kernel, depth),
-        out_shape=jax.ShapeDtypeStruct(incident.shape, bf16),
+        out_shape=pltpu.VMEM(incident.shape, bf16),
         in_specs=[smem] * 5 + [any_space] * 4,
-        out_specs=any_space,
+        out_specs=pl.BlockSpec(memory_space=pltpu.VMEM),
         scratch_shapes=[
             pltpu.VMEM((waves, row_count, tile_rows, columns), bf16),
             pltpu.VMEM((waves, 4, tile_rows, columns), bf16),
@@ -703,7 +697,6 @@
             pltpu.VMEM((places + 1, waves, row_blocks, 2, rank_rows, tile_rows), bf16),
             pltpu.VMEM((places + 1, waves, row_blocks, rank_rows, columns), bf16),
             pltpu.VMEM((waves, 2 * tile_rows, columns), f32),
-            pltpu.VMEM(incident.shape, bf16),
             pltpu.SMEM((slots,), jnp.int32),
             pltpu.SMEM((2, row_blocks, row_count), jnp.int32),
             dma((waves, row_count + 2)),
@@ -718,7 +711,6 @@
             dma((1,)),
             dma((depth,)),
             dma((3 + waves,)),
-            dma((waves,)),
         ],
         compiler_params=pltpu.CompilerParams(collective_id=0, has_side_effects=True),
     )(near_offsets, far_row, far_col, far_rank, far_count, incident, near_tiles, far_u, far_v)

time: 63.1 us -> 58 us (0.919)
  Pallas kernels: 60.1 us -> 56.3 us
  local copies, waits for them, and re-layouts: 1.87 us -> 0.8 us
    pallas_call x1, Pallas kernels: 60.1 us -> 56.3 us  [fused_shards(): pl.pallas_call(functools.partial(fused_kernel, depth), out_shape=pltpu.VM...]
    unnamed x1, local copies, waits for them, and re-layouts: 1.87 us -> 0.8 us
where the time goes in v3:
time: 58 us; the launch traced here: 57.7 us
  Pallas kernels  56.3 us (97%)
  local copies, waits for them, and re-layouts  0.8 us (1%)
  between operations  0.66 us (1%)
    pallas_call x1, Pallas kernels, fused_shards(): pl.pallas_call(functools.partial(fused_kernel, depth), out_shape=pltpu.VM...  56.3 us

profile of v3, /device:TPU:0, one launch (start us, length us, event | category | flops | bytes accessed | tf_op | source)
XLA Modules:
  0.0 57.7 jit_solution(11720147811689888475)
XLA Ops:
  0.7 56.3 %shard_map.91 = bf16[2,256,512]{2,1,0:T(8,128)(2,1)S(1)} custom-call(s32[1,3]{1,0:T(1,128)} %offset_ref.1, s32[1,1,16]{2,1,0:T(1,128)} %row_ref.1, s32[1,1,16]{2,1,0:T(1,128)} %col_ref.1, s32[1,1,16]{2,1,0:T(1,128)} %rank_ref.1, s32[1,1]{1,0:T(1,128)S(6)} %copy.12.count_ref, bf16[2,256,512]{2,1,0:T(8,128)(2,1)} %x_hbm.1, ...), custom_call_target="tpu_custom_call" | custom-call | tf_op jit(solution)/shard_map/pallas_call | solution.py:681
  56.9 0.8 %copy.11 = bf16[2,256,512]{2,1,0:T(8,128)(2,1)} copy(bf16[2,256,512]{2,1,0:T(8,128)(2,1)S(1)} %shard_map.91) | data formatting | bytes 1048576

commit v4 on v3

--- a/solution.py
+++ b/solution.py
@@ -131,8 +131,8 @@
 
 
 def fused_kernel(
-    depth, offset_ref, row_ref, col_ref, rank_ref, count_ref, x_hbm, near_hbm, u_hbm, v_hbm, out_ref,
-    tiles, close, near_buf, u_buf, v_buf, u_turn, u_give, coef, give, v_out, v_in, served, total, keys, table,
+    depth, offset_hbm, row_hbm, col_hbm, rank_hbm, count_hbm, x_hbm, near_hbm, u_hbm, v_hbm, out_ref,
+    tiles, close, near_buf, u_buf, v_buf, u_turn, u_give, coef, give, v_out, v_in, served, total, offset_ref, row_ref, col_ref, rank_ref, count_ref, keys, table,
     recv_sem, send_sem, pair_sem, v_send, v_recv, s_send, s_recv, g_send, g_recv, t_send, t_recv, load_sem,
 ):
     waves = tiles.shape[0]
@@ -182,7 +182,15 @@
     load_v = pltpu.make_async_copy(v_hbm.at[0, 0], v_buf, load_sem.at[0])
     load_u = pltpu.make_async_copy(u_hbm.at[0, 0], u_buf, load_sem.at[1])
     load_near = pltpu.make_async_copy(near_hbm.at[0], near_buf, load_sem.at[2])
-    for load in load_x + [load_v, load_u, load_near]:
+    small = (
+        (row_hbm, row_ref), (col_hbm, col_ref), (rank_hbm, rank_ref),
+        (count_hbm, count_ref), (offset_hbm, offset_ref),
+    )
+    load_small = [
+        pltpu.make_async_copy(source, target, load_sem.at[3 + waves + n])
+        for n, (source, target) in enumerate(small)
+    ]
+    for load in load_small + load_x + [load_v, load_u, load_near]:
         load.start()
 
     barrier = pltpu.get_barrier_semaphore()
@@ -205,6 +213,8 @@
     def _():
         greet((row_of(z - 1, y, x), c))
 
+    for load in load_small:
+        load.wait()
     for s in range(slots):
         key = row_ref[0, 0, s] * row_count + col_ref[0, 0, s]
         keys[s] = jnp.where(s < count_ref[0, 0], key, -1)
@@ -574,12 +584,9 @@
             for wave in range(waves):
                 use_tile(0, r, wave)
 
-        @pl.when((distance == depth) & ~at_wrap(r))
+        @pl.when((distance == depth) & serves_side(r))
         def _():
             use_corner()
-            await_near()
-            await_first()
-            lax.fori_loop(0, waves, functools.partial(first_sum, True), 0)
 
         @pl.when(distance > 0)
         def _():
@@ -617,6 +624,16 @@
         return carry
 
     lax.fori_loop(0, depth + 1, spread, 0)
+
+    @pl.when(~at_wrap(r) & ~serves_side(r))
+    def _():
+        use_corner()
+
+    @pl.when(~at_wrap(r))
+    def _():
+        await_near()
+        await_first()
+        lax.fori_loop(0, waves, functools.partial(first_sum, True), 0)
 
     @pl.when(at_wrap(r))
     def _():
@@ -676,12 +693,11 @@
     depth, places, half = row_count // 4, row_count // 2, row_count // 8
     bf16, f32 = jnp.bfloat16, jnp.float32
     any_space = pl.BlockSpec(memory_space=pl.ANY)
-    smem = pl.BlockSpec(memory_space=pltpu.SMEM)
     dma = pltpu.SemaphoreType.DMA
     return pl.pallas_call(
         functools.partial(fused_kernel, depth),
         out_shape=pltpu.VMEM(incident.shape, bf16),
-        in_specs=[smem] * 5 + [any_space] * 4,
+        in_specs=[any_space] * 9,
         out_specs=pl.BlockSpec(memory_space=pltpu.VMEM),
         scratch_shapes=[
             pltpu.VMEM((waves, row_count, tile_rows, columns), bf16),
@@ -697,6 +713,11 @@
             pltpu.VMEM((places + 1, waves, row_blocks, 2, rank_rows, tile_rows), bf16),
             pltpu.VMEM((places + 1, waves, row_blocks, rank_rows, columns), bf16),
             pltpu.VMEM((waves, 2 * tile_rows, columns), f32),
+            pltpu.SMEM(near_offsets.shape, jnp.int32),
+            pltpu.SMEM(far_row.shape, jnp.int32),
+            pltpu.SMEM(far_col.shape, jnp.int32),
+            pltpu.SMEM(far_rank.shape, jnp.int32),
+            pltpu.SMEM(far_count.shape, jnp.int32),
             pltpu.SMEM((slots,), jnp.int32),
             pltpu.SMEM((2, row_blocks, row_count), jnp.int32),
             dma((waves, row_count + 2)),
@@ -710,7 +731,7 @@
             dma((half + 1,)),
             dma((1,)),
             dma((depth,)),
-            dma((3 + waves,)),
+            dma((8 + waves,)),
         ],
         compiler_params=pltpu.CompilerParams(collective_id=0, has_side_effects=True),
     )(near_offsets, far_row, far_col, far_rank, far_count, incident, near_tiles, far_u, far_v)

time: 58 us -> 57.4 us (0.990)
  Pallas kernels: 56.3 us -> 55.6 us
    pallas_call x1, Pallas kernels: 56.3 us -> 55.6 us  [fused_shards(): pl.pallas_call(functools.partial(fused_kernel, depth), out_shape=pltpu.VM...]
where the time goes in v4:
time: 57.4 us; the launch traced here: 57.1 us
  Pallas kernels  55.6 us (97%)
  local copies, waits for them, and re-layouts  0.8 us (1%)
  between operations  0.66 us (1%)
    pallas_call x1, Pallas kernels, fused_shards(): pl.pallas_call(functools.partial(fused_kernel, depth), out_shape=pltpu.VM...  55.6 us

profile of v4, /device:TPU:0, one launch (start us, length us, event | category | flops | bytes accessed | tf_op | source)
XLA Modules:
  0.0 57.1 jit_solution(4468095244999464388)
XLA Ops:
  0.7 55.6 %shard_map.91 = bf16[2,256,512]{2,1,0:T(8,128)(2,1)S(1)} custom-call(s32[1,3]{1,0:T(1,128)} %offset_hbm.1, s32[1,1,16]{2,1,0:T(1,128)} %row_hbm.1, s32[1,1,16]{2,1,0:T(1,128)} %col_hbm.1, s32[1,1,16]{2,1,0:T(1,128)} %rank_hbm.1, s32[1,1]{1,0:T(1,128)S(6)} %copy.12.count_hbm, bf16[2,256,512]{2,1,0:T(8,128)(2,1)} %x_hbm.1, ...), custom_call_target="tpu_custom_call" | custom-call | tf_op jit(solution)/shard_map/pallas_call | solution.py:697
  56.3 0.8 %copy.11 = bf16[2,256,512]{2,1,0:T(8,128)(2,1)} copy(bf16[2,256,512]{2,1,0:T(8,128)(2,1)S(1)} %shard_map.91) | data formatting | bytes 1048576

commit v5 on v4

--- a/solution.py
+++ b/solution.py
@@ -515,9 +515,9 @@
         across_chip = jnp.where(offset == 1 - 2 * c, 2, 3)
         return jnp.where(offset % 2 == 0, jnp.where(offset == 2 * (beside - r), 0, 1), across_chip)
 
-    def near_sum(wave):
+    def near_sum(wave, slots_used):
         value = None
-        for n in range(near_buf.shape[1]):
+        for n in slots_used:
             left = near_buf[wave, n].reshape(2 * tile_rows, tile_rows)
             block = close[wave, place_of(offset_ref[0, n])] if n else tiles[wave, r]
             prod = jnp.dot(left, block, preferred_element_type=jnp.float32)
@@ -559,14 +559,14 @@
             await_chunk(chunk)
 
     def first_sum(with_near, wave, carry):
-        value = near_sum(wave) if with_near else jnp.zeros(total.shape[1:], jnp.float32)
+        value = near_sum(wave, range(near_buf.shape[1]) if with_near else (0,))
         for chunk in range(half - 1):
             value += far_chunk(chunk, wave)
         total[wave] = value
         return carry
 
     def add_near(wave, carry):
-        total[wave] += near_sum(wave)
+        total[wave] += near_sum(wave, range(1, near_buf.shape[1]))
         return carry
 
     def comes_early(step):

time: 57.4 us -> 57.4 us (level)
  no operation moved by 1% of the time
where the time goes in v5:
time: 57.4 us; the launch traced here: 56.8 us
  Pallas kernels  55.4 us (97%)
  local copies, waits for them, and re-layouts  0.8 us (1%)
  between operations  0.66 us (1%)
    pallas_call x1, Pallas kernels, fused_shards(): pl.pallas_call(functools.partial(fused_kernel, depth), out_shape=pltpu.VM...  55.4 us

profile of v5, /device:TPU:0, one launch (start us, length us, event | category | flops | bytes accessed | tf_op | source)
XLA Modules:
  0.0 56.8 jit_solution(2224712225052851227)
XLA Ops:
  0.7 55.4 %shard_map.91 = bf16[2,256,512]{2,1,0:T(8,128)(2,1)S(1)} custom-call(s32[1,3]{1,0:T(1,128)} %offset_hbm.1, s32[1,1,16]{2,1,0:T(1,128)} %row_hbm.1, s32[1,1,16]{2,1,0:T(1,128)} %col_hbm.1, s32[1,1,16]{2,1,0:T(1,128)} %rank_hbm.1, s32[1,1]{1,0:T(1,128)S(6)} %copy.12.count_hbm, bf16[2,256,512]{2,1,0:T(8,128)(2,1)} %x_hbm.1, ...), custom_call_target="tpu_custom_call" | custom-call | tf_op jit(solution)/shard_map/pallas_call | solution.py:697
  56.0 0.8 %copy.11 = bf16[2,256,512]{2,1,0:T(8,128)(2,1)} copy(bf16[2,256,512]{2,1,0:T(8,128)(2,1)S(1)} %shard_map.91) | data formatting | bytes 1048576
